TPU v7x, 32 devices: a whole 2x2x4 slice. The times are simulated.
32 devices in a mesh: dp: 4 (over y, x), mp: 8 (over z, core).
Axes of the slice: x: 2, y: 2, z: 4, core: 2. Of those that a mesh axis runs over, the one named last changes fastest.
Arguments:
- image: bfloat16 [4, 2048, 1280], P('dp', 'mp'), may hold values from -6 to 6
- ln_gain: float32 [1280], replicated, may hold values from 0.1 to 1.9
- fc1_weight: bfloat16 [1280, 5120], P(None, ('dp', 'mp')), may hold values from -0.15625 to 0.15625
- fc2_weight: bfloat16 [5120, 1280], P(('dp', 'mp')), may hold values from -0.078125 to 0.078125
- projector_weight: bfloat16 [1280, 8192], P(None, 'mp'), may hold values from -0.15625 to 0.15625
- kv_weight: bfloat16 [8192, 8, 2, 128], P('mp'), may hold values from -0.0625 to 0.0625
- text: bfloat16 [4, 128, 8192], P('dp'), may hold values from -480 to 480
- q_weight: bfloat16 [8192, 8192], P(None, 'mp'), may hold values from -0.0625 to 0.0625
- o_weight: bfloat16 [8192, 8192], P('mp'), may hold values from -0.0625 to 0.0625
- tile_count: int32 [4], P('dp'), may hold values from 1 to 4
- text_start: int32 [4], P('dp'), may hold values from 0 to 63
Outputs:
- attended: bfloat16 [4, 128, 8192], P('dp', 'mp')
All inputs are finite; a program needn't handle non-finite values.
Results may differ from a plain program's by a relative error of at most 0.035.
Values may be sent and summed in bfloat16 or wider, within the bound.
A program may use at most 128 MiB of HBM per device.

v0:
```python
import jax
import jax.numpy as jnp
from jax import lax
from jax.sharding import PartitionSpec as P

HEAD_DIM = 128
TILE_TOK = 512


def swapped(block, axis, bit):
    count = lax.axis_size(axis)
    route = []
    for low in range(count):
        high = low | 1 << bit
        if high != low and high < count:
            route += [(low, high), (high, low)]
    return lax.ppermute(block, axis, route)


def layer_norm(values, gain):
    center = values - jnp.mean(values, axis=-1, keepdims=True)
    spread = jnp.mean(center * center, axis=-1, keepdims=True)
    return center * lax.rsqrt(spread + 1e-05) * gain


def attend_block(block_queries, keys, values, valid, scale, layout):
    scores = (
        jnp.einsum(
            "thd," + layout + "->htk", block_queries, keys, preferred_element_type=jnp.float32
        )
        * scale
    )
    scores = jnp.where(valid[None, None, :], scores, -1e30)
    top = jnp.max(scores, axis=-1, keepdims=True)
    weights = jnp.exp(scores - top)
    probs = (weights / jnp.sum(weights, axis=-1, keepdims=True)).astype(jnp.bfloat16)
    return jnp.einsum("htk," + layout + "->thd", probs, values, preferred_element_type=jnp.float32)


def local(
    image,
    ln_gain,
    fc1_weight,
    fc2_weight,
    projector_weight,
    kv_weight,
    text,
    q_weight,
    o_weight,
    tile_count,
    text_start,
):
    inputs = image[0].astype(jnp.float32)
    normed = layer_norm(inputs, ln_gain).astype(jnp.bfloat16)
    hidden = jax.nn.gelu(
        jnp.dot(
            normed,
            lax.all_gather(fc1_weight, ("dp", "mp"), axis=1, tiled=True),
            preferred_element_type=jnp.float32,
        ),
        approximate=False,
    ).astype(jnp.bfloat16)
    branch = jnp.dot(
        hidden,
        lax.all_gather(fc2_weight, ("dp", "mp"), axis=0, tiled=True),
        preferred_element_type=jnp.float32,
    )
    encoded = (inputs + branch).astype(jnp.bfloat16)
    features = jnp.dot(
        lax.all_gather(encoded, "mp", axis=0, tiled=True),
        projector_weight,
        preferred_element_type=jnp.float32,
    ).astype(jnp.bfloat16)
    image_rows = features.shape[0]
    group_count = lax.axis_size("mp")
    kv_count = kv_weight.shape[1]
    devices_per_kv = group_count // kv_count
    kv_columns = kv_count * 2 * HEAD_DIM
    flat_kv = kv_weight.reshape(kv_weight.shape[0], kv_columns)
    column_count = kv_columns // group_count
    selected = flat_kv
    portion = lax.psum_scatter(
        jnp.einsum("kf,fc->ck", features, selected, preferred_element_type=jnp.float32),
        "mp",
        scatter_dimension=0,
        tiled=True,
    )
    block_count = column_count // HEAD_DIM
    portion = portion.reshape(block_count, HEAD_DIM, image_rows)
    first_block = lax.axis_index("mp") * block_count
    is_key = (first_block + jnp.arange(block_count, dtype=jnp.int32)) % 2 == 0
    key_scale = lax.rsqrt(jnp.mean(portion * portion, axis=1, keepdims=True) + 1e-06)
    portion = jnp.where(is_key[:, None, None], portion * key_scale, portion).astype(jnp.bfloat16)
    for bit_index in range(devices_per_kv.bit_length() - 1):
        partner = swapped(portion, "mp", bit_index)
        is_lower = lax.axis_index("mp") // (1 << bit_index) % 2 == 0
        portion = jnp.where(
            is_lower, jnp.concatenate([portion, partner], 0), jnp.concatenate([partner, portion], 0)
        )
    keys = portion[0]
    values = portion[1]
    layout = "dk"
    text_rows = text.shape[1]
    local_heads = q_weight.shape[1] // HEAD_DIM
    queries = jnp.dot(text[0], q_weight, preferred_element_type=jnp.float32).astype(jnp.bfloat16)
    queries = queries.reshape(text_rows, local_heads, HEAD_DIM)
    valid = jnp.arange(image_rows, dtype=jnp.int32) // TILE_TOK < tile_count[0]
    scale = 1.0 / HEAD_DIM**0.5
    block_rows = min(text_rows, 256)
    blocks = queries.reshape(text_rows // block_rows, block_rows, local_heads, HEAD_DIM)
    attended_heads = lax.map(
        lambda block_queries: attend_block(block_queries, keys, values, valid, scale, layout),
        blocks,
    )
    attended_heads = attended_heads.reshape(text_rows, local_heads * HEAD_DIM)
    row_mask = (jnp.arange(text_rows, dtype=jnp.int32) >= text_start[0]).astype(jnp.float32)
    heads_out = (attended_heads * row_mask[:, None]).astype(jnp.bfloat16)
    selected = lax.slice_in_dim(
        heads_out, 0, text_rows // group_count * lax.axis_size("mp"), axis=0
    )
    summed_out = lax.psum_scatter(
        jnp.dot(selected, o_weight, preferred_element_type=jnp.float32).astype(jnp.bfloat16),
        "mp",
        scatter_dimension=0,
        tiled=True,
    )
    return summed_out[None]


def solution(mesh):
    return jax.shard_map(
        local,
        mesh=mesh,
        in_specs=(
            P("dp", "mp", None),
            P(),
            P(None, ("dp", "mp")),
            P(("dp", "mp"), None),
            P(None, "mp"),
            P("mp", None, None, None),
            P("dp", None, None),
            P(None, "mp"),
            P("mp", None),
            P("dp"),
            P("dp"),
        ),
        out_specs=P("dp", "mp", None),
        check_vma=False,
    )
```

profile of v0, /device:TPU:0, one launch (start us, length us, event | category | flops | bytes accessed | tf_op | source)
XLA Modules:
  0.0 553.4 jit_solution(9801383821022920745)
XLA Ops:
  6.5 0.0 copy-start
  6.5 0.0 all-gather.4.cloned.1.call-start
  6.5 0.7 all-gather.4.cloned.1.call-update
  7.3 0.0 all-gather.6.cloned.1.call-start
  7.3 0.7 all-gather.6.cloned.1.call-update
  8.0 0.0 all-gather.8.cloned.1.call-start
  8.1 1.3 convert_reduce_fusion
  9.3 1.4 fusion.62
  10.7 99.9 %all-gather.4.cloned.1.call-done = bf16[1280,5120]{0,1:T(8,128)(2,1)} async-done(((bf16[1280,160]{0,1:T(8,128)(2,1)}), bf16[1280,5120]{0,1:T(8,128)(2,1)}) %all-gather.4.cloned.1.call-update) | async-done | bytes 13107216 | tf_op jit(solution)/shard_map/all_gather | solution.py:58
  110.7 99.2 %all-gather.6.cloned.1.call-done = bf16[5120,1280]{1,0:T(8,128)(2,1)} async-done(((bf16[160,1280]{1,0:T(8,128)(2,1)}), bf16[5120,1280]{1,0:T(8,128)(2,1)}) %all-gather.6.cloned.1.call-update) | async-done | bytes 13107216 | tf_op jit(solution)/shard_map/all_gather | solution.py:65
  209.8 26.5 %fusion.51 = bf16[256,1280]{1,0:T(8,128)(2,1)} fusion(bf16[5120,1280]{1,0:T(8,128)(2,1)} %all-gather.6.cloned.1.call-done, bf16[1,256,1280]{2,1,0:T(8,128)(2,1)} %param.11, bf16[1280,5120]{0,1:T(8,128)(2,1)} %all-gather.4.cloned.1.call-done, f32[1280]{0:T(1024)} %param.12, f32[256]{0:T(256)S(1)} %add_rsqrt_fusion.1, f32[256]{0:T(256)S(1)} %broadcast_multiply_fusion), kind=kOutput, calls=%fused_computation.65 | convolution fusion | flops 6798704640 | bytes 27532288 | tf_op jit(solution)/shard_map/dot_general | solution.py:63
  236.3 0.0 all-gather.8.cloned.1.call-update
  236.4 0.2 reduce-scatter.3.cloned.1.call-start
  236.6 8.0 %reshape.70 = bf16[1024,2048]{1,0:T(8,128)(2,1)} reshape(bf16[1024,8,2,128]{3,2,1,0:T(2,128)(2,1)} %param.16) | data formatting | bytes 8388608 | tf_op jit(solution)/shard_map/reshape | solution.py:79
  244.6 46.5 %all-gather.8.cloned.1.call-done = bf16[2048,1280]{1,0:T(8,128)(2,1)} async-done(((bf16[256,1280]{1,0:T(8,128)(2,1)}), bf16[2048,1280]{1,0:T(8,128)(2,1)}) %all-gather.8.cloned.1.call-update) | async-done | bytes 5242896 | tf_op jit(solution)/shard_map/all_gather | solution.py:70
  291.0 0.0 copy-done
  291.0 20.6 %convolution_bitcast_fusion = f32[2048,2048]{0,1:T(8,128)} fusion(bf16[1024,2048]{1,0:T(8,128)(2,1)} %reshape.70, bf16[2048,1280]{1,0:T(8,128)(2,1)} %all-gather.8.cloned.1.call-done, bf16[1280,1024]{1,0:T(8,128)(2,1)S(1)} %copy-done), kind=kOutput, calls=%fused_computation.2 | convolution fusion | flops 13960740864 | bytes 28835840 | tf_op jit(solution)/shard_map/kf,fc->ck/dot_general | solution.py:83
  311.7 0.0 copy-start.3
  311.7 0.0 reduce-scatter.3.cloned.1.call-update
  311.7 0.0 reduce-scatter.5.cloned.1.call-start
  313.2 0.1 copy-done.3
  313.3 8.9 %fusion.68 = bf16[16,8,8,128]{3,2,1,0:T(8,128)(2,1)S(1)} fusion(bf16[8192,1024]{1,0:T(8,128)(2,1)} %param.18, bf16[1,128,8192]{2,1,0:T(8,128)(2,1)S(1)} %copy-done.3), kind=kOutput, calls=%fused_computation.80 | convolution fusion | flops 2147614720 | bytes 19136512 | tf_op jit(solution)/shard_map/dot_general | solution.py:105
  322.2 156.6 %reduce-scatter.3.cloned.1.call-done = f32[256,2048]{0,1:T(8,128)} async-done(((f32[2048,2048]{0,1:T(8,128)}), f32[256,2048]{0,1:T(8,128)}) %reduce-scatter.3.cloned.1.call-update) | async-done | bytes 2097168 | tf_op jit(solution)/shard_map/reduce_scatter | solution.py:82
  478.8 0.0 copy-start.2
  478.8 3.5 reshape.71
  482.2 5.7 %multiply_reduce_fusion = f32[2,2048]{0,1:T(8,128)} fusion(f32[2,128,2048]{1,0,2:T(2,128)} %reshape.71), kind=kLoop, calls=%fused_computation.69 | loop fusion | flops 1044480 | bytes 2113536 | tf_op jit(solution)/shard_map/reduce_sum | solution.py:92
  487.9 1.6 copy.23
  489.5 0.0 copy-done.2
  489.5 1.6 fusion.54
  491.1 0.0 copy-start.4
  491.1 7.1 %fusion.133 = (f32[8,128]{1,0:T(8,128)S(1)}, f32[8,128,2048]{1,2,0:T(8,128)}) fusion(pred[2048]{0:T(1024)(128)(4,1)S(1)} %fusion.95, bf16[2,128,2048]{1,2,0:T(8,128)(2,1)} %fusion.54, bf16[16,8,8,128]{3,2,1,0:T(8,128)(2,1)S(1)} %fusion.68), kind=kOutput, calls=%fused_computation.144 | convolution fusion | flops 545261568 | bytes 9181184 | tf_op jit(solution)/shard_map/while/body/eval_jaxpr/sub | solution.py:35
  498.2 0.0 copy-done.4
  498.2 4.1 fusion.19
  502.4 0.0 copy-start.1
  502.4 9.7 %convolution_convert_fusion = bf16[128,8192]{1,0:T(8,128)(2,1)} fusion(bf16[128,1024]{0,1:T(8,128)(2,1)S(1)} %fusion.85, bf16[1024,8192]{1,0:T(8,128)(2,1)} %param.19), kind=kOutput, calls=%fused_computation.1 | convolution fusion | flops 2148532224 | bytes 19136512 | tf_op jit(solution)/shard_map/dot_general | solution.py:122
  512.1 0.0 reduce-scatter.5.cloned.1.call-update
  512.2 34.7 %reduce-scatter.5.cloned.1.call-done = bf16[16,8192]{1,0:T(8,128)(2,1)} async-done(((bf16[128,8192]{1,0:T(8,128)(2,1)}), bf16[16,8192]{1,0:T(8,128)(2,1)}) %reduce-scatter.5.cloned.1.call-update) | async-done | bytes 262160 | tf_op jit(solution)/shard_map/reduce_scatter | solution.py:121
  546.8 0.0 copy-done.1
  (7 shorter events, 0.1 us)
Async XLA Ops:
  6.5 284.5 %copy-start = (bf16[1280,1024]{1,0:T(8,128)(2,1)S(1)}, bf16[1280,1024]{1,0:T(8,128)(2,1)}, u32[]{:S(2)}) copy-start(bf16[1280,1024]{1,0:T(8,128)(2,1)} %param.15) | copy-start | bytes 7864324
  6.5 104.1 %all-gather.4.cloned.1.call-start = ((), (), s32[]{:S(2)}) async-start(), calls=%async_computation.2 | async-start | bytes 13516800 | tf_op jit(solution)/shard_map/all_gather | solution.py:58
  7.3 202.6 %all-gather.6.cloned.1.call-start = ((), (), s32[]{:S(2)}) async-start(), calls=%async_computation.3 | async-start | bytes 13516800 | tf_op jit(solution)/shard_map/all_gather | solution.py:65
  8.0 283.0 %all-gather.8.cloned.1.call-start = ((), (), s32[]{:S(2)}) async-start(), calls=%async_computation.4 | async-start | bytes 5898240 | tf_op jit(solution)/shard_map/all_gather | solution.py:70
  236.4 242.4 %reduce-scatter.3.cloned.1.call-start = ((), (), s32[]{:S(2)}) async-start(), calls=%async_computation.5 | async-start | bytes 18874368 | tf_op jit(solution)/shard_map/reduce_scatter | solution.py:82
  311.7 1.6 copy-start.3
  311.7 235.1 %reduce-scatter.5.cloned.1.call-start = ((), (), s32[]{:S(2)}) async-start(), calls=%async_computation.6 | async-start | bytes 2359296 | tf_op jit(solution)/shard_map/reduce_scatter | solution.py:121
  478.8 10.7 %copy-start.2 = (f32[256,2048]{0,1:T(8,128)S(1)}, f32[256,2048]{0,1:T(8,128)}, u32[]{:S(2)}) copy-start(f32[256,2048]{0,1:T(8,128)} %reduce-scatter.3.cloned.1.call-done) | copy-start | bytes 6291460
  491.1 7.1 %copy-start.4 = (bf16[2,128,2048]{1,2,0:T(8,128)(2,1)S(1)}, bf16[2,128,2048]{1,2,0:T(8,128)(2,1)}, u32[]{:S(2)}) copy-start(bf16[2,128,2048]{1,2,0:T(8,128)(2,1)} %fusion.54) | copy-start | bytes 3145732
  502.4 44.5 %copy-start.1 = (bf16[1280,1024]{1,0:T(8,128)(2,1)S(1)}, bf16[1280,1024]{1,0:T(8,128)(2,1)}, u32[]{:S(2)}) copy-start(bf16[1280,1024]{1,0:T(8,128)(2,1)} %param.15) | copy-start | bytes 7864324
Sparse Core Ops, SparseCore 0:
  10.2 100.4 all-gather.3
  113.5 96.2 all-gather.5
  236.5 54.5 all-gather.7
  311.8 166.9 reduce-scatter.2
  512.3 34.5 reduce-scatter.4
where the time goes:
time: 554 us; the launch traced here: 553 us
  waiting for transfers between devices  438 us (79%)
  matrix products  77 us (14%)
  between operations  14.7 us (3%)
  local copies, waits for them, and re-layouts  13 us (2%)
  other arithmetic  10 us (2%)
    reduce_scatter x1, waiting for transfers between devices, local(): lax.psum_scatter(jnp.einsum('kf,fc->ck', features, selected, preferred_el...  157 us
    all_gather x1, waiting for transfers between devices, local(): lax.all_gather(fc1_weight, ('dp', 'mp'), axis=1, tiled=True)  99.9 us
    all_gather x1, waiting for transfers between devices, local(): lax.all_gather(fc2_weight, ('dp', 'mp'), axis=0, tiled=True)  99.2 us
    all_gather x1, waiting for transfers between devices, local(): lax.all_gather(encoded, 'mp', axis=0, tiled=True)  46.5 us
    reduce_scatter x1, waiting for transfers between devices, local(): lax.psum_scatter(jnp.dot(selected, o_weight, preferred_element_type=jnp.f...  34.7 us
    dot_general x1, matrix products, local(): jnp.dot(hidden, lax.all_gather(fc2_weight, ('dp', 'mp'), axis=0, tiled=Tr...  26.5 us
    dot_general x1, matrix products, local(): jnp.einsum('kf,fc->ck', features, selected, preferred_element_type=jnp.fl...  20.6 us
  transfers between devices with their start and end apart: 5, of which 5 were waited for; matrix products, arithmetic and copies ran while one was open for 4% of the time, Pallas kernels for 0%

commit v1 on v0

v1 whole, which is shorter than its diff:
```python
import functools

import jax
import jax.numpy as jnp
from jax import lax
from jax.experimental import pallas as pl
from jax.experimental.pallas import tpu as pltpu
from jax.sharding import PartitionSpec as P

HEAD_DIM = 128
TILE_TOK = 512

MESH = pl.DeviceIdType.MESH
CORES = 2


def count_copies(kind):
    name, axis = kind
    size = lax.axis_size(axis)
    if name == "chain":
        return 2 * (size // CORES - 1) + size // CORES
    if name == "partner":
        return size // CORES
    if name == "stride":
        return size // CORES - 1
    return size - 1


def exchange_kernel(kinds, *refs):
    count = len(kinds)
    sources, results = refs[:count], refs[count : 2 * count]
    local_sem = refs[2 * count]
    sends, recvs = refs[2 * count + 1 : 3 * count + 1], refs[3 * count + 1 :]
    axes = sorted({axis for _, axis in kinds})

    barrier = pltpu.get_barrier_semaphore()
    greeted = 0
    for axis in axes:
        size, me = lax.axis_size(axis), lax.axis_index(axis)
        for step in range(1, size):
            pl.semaphore_signal(
                barrier, inc=1, device_id={axis: lax.rem(me + step, size)}, device_id_type=MESH
            )
        greeted += size - 1
    pl.semaphore_wait(barrier, greeted)

    def remote(op, source, result, slot, axis, peer):
        return pltpu.make_async_remote_copy(
            src_ref=source,
            dst_ref=result,
            send_sem=sends[op].at[slot],
            recv_sem=recvs[op].at[slot],
            device_id={axis: peer},
            device_id_type=MESH,
        )

    simple, chains, locals_ = [], [], []
    for op, (name, axis) in enumerate(kinds):
        size, me = lax.axis_size(axis), lax.axis_index(axis)
        source, result = sources[op], results[op]
        core = lax.rem(me, CORES)
        spot = lax.div(me, CORES)
        partner = me + 1 - 2 * core
        if name == "gather":
            for step in range(1, size):
                copy = remote(op, source, result.at[me], step - 1, axis, lax.rem(me + step, size))
                copy.start()
                simple.append(copy)
            locals_.append(pltpu.make_async_copy(source, result.at[me], local_sem.at[op]))
        elif name == "columns":
            width = result.shape[-1]

            def column(index):
                return source.at[:, pl.ds(pl.multiple_of(index * width, width), width)]

            for step in range(1, size):
                peer = lax.rem(me + step, size)
                copy = remote(op, column(peer), result.at[me], step - 1, axis, peer)
                copy.start()
                simple.append(copy)
            locals_.append(pltpu.make_async_copy(column(me), result.at[me], local_sem.at[op]))
        elif name == "scatter":
            for step in range(1, size):
                peer = lax.rem(me + step, size)
                copy = remote(op, source.at[peer], result.at[me], step - 1, axis, peer)
                copy.start()
                simple.append(copy)
            locals_.append(pltpu.make_async_copy(source.at[me], result.at[me], local_sem.at[op]))
        elif name == "partner":
            for chip in range(size // CORES):
                copy = remote(
                    op, source.at[chip * CORES + 1 - core], result.at[chip], chip, axis, partner
                )
                copy.start()
                simple.append(copy)
        elif name == "stride":
            chips = size // CORES
            for step in range(1, chips):
                other = lax.rem(spot + step, chips)
                copy = remote(
                    op, source.at[other], result.at[spot], step - 1, axis, other * CORES + core
                )
                copy.start()
                simple.append(copy)
            locals_.append(pltpu.make_async_copy(source.at[spot], result.at[spot], local_sem.at[op]))
        else:
            chains.append((op, axis, size // CORES, me, core, spot, partner, source, result))
    for copy in locals_:
        copy.start()

    def hop(chain, source, block, slot, peer):
        op, axis, result = chain[0], chain[1], chain[-1]
        return remote(op, source, result.at[block], slot, axis, peer)

    for chain in chains:
        op, axis, chips, me, core, spot, partner, source, result = chain

        @pl.when(spot + 1 < chips)
        def _():
            hop(chain, source, me, 0, me + CORES).start()

        @pl.when(spot > 0)
        def _():
            hop(chain, source, me, chips - 1, me - CORES).start()

    for chain in chains:
        op, axis, chips, me, core, spot, partner, source, result = chain
        hop(chain, source, me, 2 * (chips - 1), partner).start()
        pltpu.make_async_copy(source, result.at[me], local_sem.at[op]).start()
    for step in range(1, max([chain[2] for chain in chains], default=0)):
        for chain in chains:
            op, axis, chips, me, core, spot, partner, source, result = chain
            for sign, base in ((1, 0), (-1, chips - 1)):
                origin_spot = spot - sign * step
                here = (origin_spot >= 0) & (origin_spot < chips)
                onward = (spot + sign >= 0) & (spot + sign < chips)
                block = me - sign * step * CORES

                @pl.when(here)
                def _():
                    held = result.at[block]
                    hop(chain, held, block, base + step - 1, me).wait_recv()

                    @pl.when(onward)
                    def _():
                        hop(chain, held, block, base + step, me + sign * CORES).start()

                    slot = 2 * (chips - 1) + lax.rem(origin_spot - spot + chips, chips)
                    hop(chain, held, block, slot, partner).start()

    for chain in chains:
        op, axis, chips, me, core, spot, partner, source, result = chain
        for step in range(chips):
            for_spot = lax.rem(spot + step, chips)
            block = for_spot * CORES + core
            theirs = for_spot * CORES + 1 - core
            slot = 2 * (chips - 1) + step
            hop(chain, result.at[block], block, slot, partner).wait_send()
            hop(chain, result.at[theirs], theirs, slot, partner).wait_recv()
        for step in range(chips - 1):
            for sign, base in ((1, 0), (-1, chips - 1)):
                origin_spot = spot - sign * step
                sent = (
                    (origin_spot >= 0)
                    & (origin_spot < chips)
                    & (spot + sign >= 0)
                    & (spot + sign < chips)
                )
                block = me - sign * step * CORES

                @pl.when(sent)
                def _():
                    hop(chain, source, block, base + step, partner).wait_send()

        pltpu.make_async_copy(source, result.at[me], local_sem.at[op]).wait()
    for copy in simple:
        copy.wait()
    for copy in locals_:
        copy.wait()


def exchange(kinds, arrays, number):
    kinds = tuple(kinds)
    shapes = []
    for (name, axis), array in zip(kinds, arrays):
        size = lax.axis_size(axis)
        if name in ("gather", "chain"):
            shape = (size,) + array.shape
        elif name == "columns":
            shape = (size, array.shape[0], array.shape[1] // size)
        elif name == "scatter":
            shape = array.shape
        else:
            shape = (size // CORES,) + array.shape[1:]
        shapes.append(jax.ShapeDtypeStruct(shape, array.dtype))
    sems = [pltpu.SemaphoreType.DMA((count_copies(kind),)) for kind in kinds]
    return pl.pallas_call(
        functools.partial(exchange_kernel, kinds),
        out_shape=shapes,
        in_specs=[pl.BlockSpec(memory_space=pl.ANY)] * len(kinds),
        out_specs=[pl.BlockSpec(memory_space=pl.ANY)] * len(kinds),
        scratch_shapes=[pltpu.SemaphoreType.DMA((len(kinds),))] + sems + sems,
        compiler_params=pltpu.CompilerParams(collective_id=number, has_side_effects=True),
        name="exchange",
    )(*arrays)


def swapped(block, axis, bit):
    count = lax.axis_size(axis)
    route = []
    for low in range(count):
        high = low | 1 << bit
        if high != low and high < count:
            route += [(low, high), (high, low)]
    return lax.ppermute(block, axis, route)


def layer_norm(values, gain):
    center = values - jnp.mean(values, axis=-1, keepdims=True)
    spread = jnp.mean(center * center, axis=-1, keepdims=True)
    return center * lax.rsqrt(spread + 1e-05) * gain


def attend_block(block_queries, keys, values, valid, scale, layout):
    scores = (
        jnp.einsum(
            "thd," + layout + "->htk", block_queries, keys, preferred_element_type=jnp.float32
        )
        * scale
    )
    scores = jnp.where(valid[None, None, :], scores, -1e30)
    top = jnp.max(scores, axis=-1, keepdims=True)
    weights = jnp.exp(scores - top)
    probs = (weights / jnp.sum(weights, axis=-1, keepdims=True)).astype(jnp.bfloat16)
    return jnp.einsum("htk," + layout + "->thd", probs, values, preferred_element_type=jnp.float32)


def local(
    image,
    ln_gain,
    fc1_weight,
    fc2_weight,
    projector_weight,
    kv_weight,
    text,
    q_weight,
    o_weight,
    tile_count,
    text_start,
):
    inputs = image[0].astype(jnp.float32)
    group_count = lax.axis_size("mp")
    normed = layer_norm(inputs, ln_gain).astype(jnp.bfloat16)
    up, down, all_normed = exchange(
        (("chain", "mp"), ("chain", "mp"), ("gather", "dp")), (fc1_weight.T, fc2_weight, normed), 0
    )
    up = up.reshape(-1, up.shape[-1])
    down = down.reshape(-1, down.shape[-1])
    all_normed = all_normed.reshape(-1, all_normed.shape[-1])
    hidden = jax.nn.gelu(
        lax.dot_general(
            all_normed, up, (((1,), (1,)), ((), ())), preferred_element_type=jnp.float32
        ),
        approximate=False,
    ).astype(jnp.bfloat16)
    branch = jnp.dot(hidden, down, preferred_element_type=jnp.float32).astype(jnp.bfloat16)
    branch = branch.reshape((lax.axis_size("dp"),) + inputs.shape)

    kv_count = kv_weight.shape[1]
    devices_per_kv = group_count // kv_count
    kv_columns = kv_count * 2 * HEAD_DIM
    flat_kv = kv_weight.reshape(kv_weight.shape[0], kv_columns)
    row_count = projector_weight.shape[0] // lax.axis_size("dp")
    rows = lax.dynamic_slice_in_dim(
        projector_weight, lax.axis_index("dp") * row_count, row_count, axis=0
    )
    folded = jnp.dot(rows, flat_kv, preferred_element_type=jnp.float32).astype(jnp.bfloat16)
    terms, folded = exchange((("scatter", "dp"), ("columns", "mp")), (branch, folded), 1)
    encoded = (inputs + jnp.sum(terms.astype(jnp.float32), axis=0)).astype(jnp.bfloat16)
    folded = jnp.sum(folded.astype(jnp.float32), axis=0).astype(jnp.bfloat16)
    for bit_index in range(devices_per_kv.bit_length() - 1):
        partner = swapped(folded, "mp", bit_index)
        is_lower = lax.axis_index("mp") // (1 << bit_index) % 2 == 0
        folded = jnp.where(
            is_lower, jnp.concatenate([folded, partner], 1), jnp.concatenate([partner, folded], 1)
        )
    all_encoded, folded = exchange((("chain", "mp"), ("gather", "dp")), (encoded, folded), 2)
    all_encoded = all_encoded.reshape(-1, all_encoded.shape[-1])
    folded = folded.reshape(-1, folded.shape[-1])
    image_rows = all_encoded.shape[0]
    portion = jnp.einsum("rc,kr->ck", folded, all_encoded, preferred_element_type=jnp.float32)
    keys = portion[:HEAD_DIM]
    key_scale = lax.rsqrt(jnp.mean(keys * keys, axis=0, keepdims=True) + 1e-06)
    keys = (keys * key_scale).astype(jnp.bfloat16)
    values = portion[HEAD_DIM:].astype(jnp.bfloat16)
    layout = "dk"
    text_rows = text.shape[1]
    local_heads = q_weight.shape[1] // HEAD_DIM
    queries = jnp.dot(text[0], q_weight, preferred_element_type=jnp.float32).astype(jnp.bfloat16)
    queries = queries.reshape(text_rows, local_heads, HEAD_DIM)
    valid = jnp.arange(image_rows, dtype=jnp.int32) // TILE_TOK < tile_count[0]
    scale = 1.0 / HEAD_DIM**0.5
    block_rows = min(text_rows, 256)
    blocks = queries.reshape(text_rows // block_rows, block_rows, local_heads, HEAD_DIM)
    attended_heads = lax.map(
        lambda block_queries: attend_block(block_queries, keys, values, valid, scale, layout),
        blocks,
    )
    attended_heads = attended_heads.reshape(text_rows, local_heads * HEAD_DIM)
    row_mask = (jnp.arange(text_rows, dtype=jnp.int32) >= text_start[0]).astype(jnp.float32)
    heads_out = (attended_heads * row_mask[:, None]).astype(jnp.bfloat16)
    out = jnp.dot(heads_out, o_weight, preferred_element_type=jnp.float32).astype(jnp.bfloat16)
    out = out.reshape(group_count, text_rows // group_count, out.shape[-1])
    (theirs,) = exchange((("partner", "mp"),), (out,), 3)
    chip_out = out.reshape((group_count // CORES, CORES) + out.shape[1:])
    mine = lax.dynamic_index_in_dim(
        chip_out, lax.axis_index("mp") % CORES, axis=1, keepdims=False
    )
    paired = (mine.astype(jnp.float32) + theirs.astype(jnp.float32)).astype(jnp.bfloat16)
    (terms,) = exchange((("stride", "mp"),), (paired,), 4)
    summed_out = jnp.sum(terms.astype(jnp.float32), axis=0).astype(jnp.bfloat16)
    return summed_out[None]


def solution(mesh):
    return jax.shard_map(
        local,
        mesh=mesh,
        in_specs=(
            P("dp", "mp", None),
            P(),
            P(None, ("dp", "mp")),
            P(("dp", "mp"), None),
            P(None, "mp"),
            P("mp", None, None, None),
            P("dp", None, None),
            P(None, "mp"),
            P("mp", None),
            P("dp"),
            P("dp"),
        ),
        out_specs=P("dp", "mp", None),
        check_vma=False,
    )
```

time: 554 us -> 262 us (0.47)
  waiting for transfers between devices: 438 us -> 0 us
  Pallas kernels: 0 us -> 173 us
  matrix products: 77 us -> 60 us
  between operations: 14.7 us -> 1.48 us
    all_gather x3 -> x0, waiting for transfers between devices: 246 us -> none  [the longest x1 99.9 us: local(): lax.all_gather(fc1_weight, ('dp', 'mp'), axis=1, tiled=True)]
    reduce_scatter x2 -> x0, waiting for transfers between devices: 191 us -> none  [the longest x1 157 us: local(): lax.psum_scatter(jnp.einsum('kf,fc->ck', features, selected, preferred_el...]
    pallas_call x0 -> x5, Pallas kernels: none -> 173 us  [exchange(): pl.pallas_call(functools.partial(exchange_kernel, kinds), out_shape=shape...]
    dot_general x3 -> x4, matrix products: 56.8 us -> 40.1 us  [the longest x1 21.3 us: local(): jnp.dot(hidden, down, preferred_element_type=jnp.float32)]
  transfers between devices with their start and end apart: 5 -> 0, of which waited for: 5 -> 0; matrix products, arithmetic and copies ran while one was open for 4% -> 0% of each run, Pallas kernels for 0% -> 0%
where the time goes in v1:
time: 262 us; the launch traced here: 259 us
  Pallas kernels  173 us (66%)
  matrix products  60 us (23%)
  other arithmetic  15.5 us (6%)
  local copies, waits for them, and re-layouts  9.2 us (4%)
    pallas_call x5, Pallas kernels, exchange(): pl.pallas_call(functools.partial(exchange_kernel, kinds), out_shape=shape...  173 us
    dot_general x1, matrix products, local(): jnp.dot(hidden, down, preferred_element_type=jnp.float32)  21.3 us
    dot_general x1, matrix products, local(): jnp.dot(heads_out, o_weight, preferred_element_type=jnp.float32)  9.74 us
    dot_general x1, matrix products, local(): jnp.dot(text[0], q_weight, preferred_element_type=jnp.float32)  8.1 us
    reshape x1, local copies, waits for them, and re-layouts, local(): flat_kv = kv_weight.reshape(kv_weight.shape[0], kv_columns)  7.79 us
    sub x1, matrix products, attend_block(): weights = jnp.exp(scores - top)  7.71 us

profile of v1, /device:TPU:0, one launch (start us, length us, event | category | flops | bytes accessed | tf_op | source)
XLA Modules:
  0.0 258.9 jit_solution(10231856760635636548)
XLA Ops:
  0.0 0.0 copy-start
  0.0 1.4 convert_reduce_fusion.1
  1.4 1.4 fusion.56
  2.8 2.2 fusion.58.refs_2_
  5.0 61.8 %exchange.5 = (bf16[8,160,1280]{2,1,0:T(8,128)(2,1)}, bf16[8,160,1280]{2,1,0:T(8,128)(2,1)}, bf16[4,256,1280]{2,1,0:T(8,128)(2,1)}) custom-call(bf16[160,1280]{1,0:T(8,128)(2,1)} %bitcast.101, bf16[160,1280]{1,0:T(8,128)(2,1)} %refs_1_.1, bf16[256,1280]{1,0:T(8,128)(2,1)} %fusion.58.refs_2_), custom_call_target="tpu_custom_call" | custom-call | tf_op jit(solution)/shard_map/exchange/pallas_call | solution.py:197
  66.8 21.3 %convolution_convert_fusion.1 = bf16[1024,1280]{1,0:T(8,128)(2,1)} fusion(bf16[1280,1280]{1,0:T(8,128)(2,1)} %bitcast.104, bf16[1024,1280]{1,0:T(8,128)(2,1)} %bitcast.105, bf16[1280,1280]{1,0:T(8,128)(2,1)} %bitcast.103), kind=kOutput, calls=%fused_computation.32 | convolution fusion | flops 6797393920 | bytes 11796480 | tf_op jit(solution)/shard_map/dot_general | solution.py:266
  88.1 7.8 %reshape.78 = bf16[1024,2048]{1,0:T(8,128)(2,1)} reshape(bf16[1024,8,2,128]{3,2,1,0:T(2,128)(2,1)} %param.16) | data formatting | bytes 8388608 | tf_op jit(solution)/shard_map/reshape | solution.py:272
  95.9 0.0 copy-done
  95.9 4.8 %convolution_convert_fusion.2.refs_1_ = bf16[320,2048]{1,0:T(8,128)(2,1)} fusion(bf16[1024,2048]{1,0:T(8,128)(2,1)} %reshape.78, bf16[1280,1024]{1,0:T(8,128)(2,1)S(1)} %copy-done, s32[]{:T(128)S(6)} %select_n.31), kind=kOutput, calls=%fused_computation.33 | convolution fusion | flops 1342832640 | bytes 6160388 | tf_op jit(solution)/shard_map/dot_general | solution.py:277
  100.7 0.0 copy-start.2
  100.7 32.6 %exchange.6 = (bf16[4,256,1280]{2,1,0:T(8,128)(2,1)}, bf16[8,320,256]{2,1,0:T(8,128)(2,1)}) custom-call(bf16[4,256,1280]{2,1,0:T(8,128)(2,1)} %bitcast.100, bf16[320,2048]{1,0:T(8,128)(2,1)} %convolution_convert_fusion.2.refs_1_), custom_call_target="tpu_custom_call" | custom-call | tf_op jit(solution)/shard_map/exchange/pallas_call | solution.py:197
  133.3 2.2 convert_reduce_fusion
  135.6 0.0 copy-done.2
  135.6 1.0 fusion.59.refs_0_
  136.5 2.2 reduce_sum.73.refs_1_
  138.7 0.0 copy-start.3
  138.7 51.5 %exchange.7 = (bf16[8,256,1280]{2,1,0:T(8,128)(2,1)}, bf16[4,320,256]{2,1,0:T(8,128)(2,1)}) custom-call(bf16[256,1280]{1,0:T(8,128)(2,1)} %fusion.59.refs_0_, bf16[320,256]{1,0:T(8,128)(2,1)} %reduce_sum.73.refs_1_), custom_call_target="tpu_custom_call" | custom-call | tf_op jit(solution)/shard_map/exchange/pallas_call | solution.py:197
  190.2 4.3 %fusion.136 = f32[256,2048]{1,0:T(8,128)S(1)} fusion(bf16[1280,256]{1,0:T(8,128)(2,1)} %bitcast.106, bf16[2048,1280]{1,0:T(8,128)(2,1)} %bitcast.102), kind=kOutput, calls=%fused_computation.140 | convolution fusion | flops 1342177280 | bytes 7995392 | tf_op jit(solution)/shard_map/rc,kr->ck/dot_general | solution.py:291
  194.5 0.0 copy-start.4
  194.5 1.4 copy-done.4
  195.9 0.1 multiply_reduce_fusion
  196.0 0.0 copy-done.3
  196.0 8.1 %fusion.63 = bf16[16,8,8,128]{3,2,1,0:T(8,128)(2,1)S(1)} fusion(bf16[8192,1024]{1,0:T(8,128)(2,1)} %param.18, bf16[1,128,8192]{2,1,0:T(8,128)(2,1)S(1)} %copy-done.3), kind=kOutput, calls=%fused_computation.78 | convolution fusion | flops 2147614720 | bytes 19136512 | tf_op jit(solution)/shard_map/dot_general | solution.py:299
  204.8 0.0 copy-start.5
  204.8 7.7 %fusion.125 = (f32[8,128]{1,0:T(8,128)S(1)}, f32[8,128,2048]{1,2,0:T(8,128)}) fusion(pred[2048]{0:T(1024)(128)(4,1)S(1)} %fusion.88, bf16[16,8,8,128]{3,2,1,0:T(8,128)(2,1)S(1)} %fusion.63, f32[256,2048]{1,0:T(8,128)} %copy-done.4, f32[2048]{0:T(1024)S(1)} %add_rsqrt_fusion), kind=kOutput, calls=%fused_computation.138 | convolution fusion | flops 545785856 | bytes 9713664 | tf_op jit(solution)/shard_map/while/body/eval_jaxpr/sub | solution.py:233
  212.5 0.0 copy-done.5
  212.5 4.1 %fusion.18 = f32[128,8,128]{2,0,1:T(8,128)S(1)} fusion(f32[8,128,2048]{1,2,0:T(8,128)} %get-tuple-element.38, f32[8,128]{1,0:T(8,128)S(1)} %get-tuple-element.37, f32[256,2048]{1,0:T(8,128)S(1)} %copy-done.5), kind=kOutput, calls=%fused_computation.31 | convolution fusion | flops 541065216 | bytes 9441280 | tf_op jit(solution)/shard_map/while/body/eval_jaxpr/htk,dk->thd/dot_general | solution.py:235
  217.3 0.0 copy-start.1
  217.3 9.7 %convolution_convert_fusion = bf16[128,8192]{1,0:T(8,128)(2,1)} fusion(bf16[128,1024]{0,1:T(8,128)(2,1)S(1)} %fusion.72, bf16[1024,8192]{1,0:T(8,128)(2,1)} %param.19), kind=kOutput, calls=%fused_computation.1 | convolution fusion | flops 2148532224 | bytes 19136512 | tf_op jit(solution)/shard_map/dot_general | solution.py:312
  227.1 5.1 %exchange.8 = bf16[4,16,8192]{2,1,0:T(8,128)(2,1)} custom-call(bf16[8,16,8192]{2,1,0:T(8,128)(2,1)} %bitcast.98), custom_call_target="tpu_custom_call" | custom-call | tf_op jit(solution)/shard_map/exchange/pallas_call | solution.py:197
  232.2 2.8 %fusion.49.refs_0_ = bf16[4,16,8192]{2,1,0:T(8,128)(2,1)} fusion(bf16[4,16,8192]{2,1,0:T(8,128)(2,1)} %exchange.8, bf16[4,2,16,8192]{3,2,1,0:T(8,128)(2,1)} %bitcast.99, s32[]{:T(128)S(6)} %select_n.36), kind=kLoop, calls=%fused_computation.64 | loop fusion | flops 2097152 | bytes 3145732 | tf_op jit(solution)/shard_map/convert_element_type | solution.py:319
  235.0 21.7 %exchange.9 = bf16[4,16,8192]{2,1,0:T(8,128)(2,1)} custom-call(bf16[4,16,8192]{2,1,0:T(8,128)(2,1)} %fusion.49.refs_0_), custom_call_target="tpu_custom_call" | custom-call | tf_op jit(solution)/shard_map/exchange/pallas_call | solution.py:197
  256.7 2.2 reduce_sum.76
  258.9 0.0 copy-done.1
  (6 shorter events, 0.1 us)
Async XLA Ops:
  0.0 95.9 %copy-start = (bf16[1280,1024]{1,0:T(8,128)(2,1)S(1)}, bf16[1280,1024]{1,0:T(8,128)(2,1)}, u32[]{:S(2)}) copy-start(bf16[1280,1024]{1,0:T(8,128)(2,1)} %param.15) | copy-start | bytes 7864324
  100.7 34.9 %copy-start.2 = (bf16[1,256,1280]{2,1,0:T(8,128)(2,1)S(1)}, bf16[1,256,1280]{2,1,0:T(8,128)(2,1)}, u32[]{:S(2)}) copy-start(bf16[1,256,1280]{2,1,0:T(8,128)(2,1)} %param.11) | copy-start | bytes 1966084
  138.7 57.3 %copy-start.3 = (bf16[1,128,8192]{2,1,0:T(8,128)(2,1)S(1)}, bf16[1,128,8192]{2,1,0:T(8,128)(2,1)}, u32[]{:S(2)}) copy-start(bf16[1,128,8192]{2,1,0:T(8,128)(2,1)} %param.17) | copy-start | bytes 6291460
  194.5 1.4 copy-start.4
  204.8 7.7 %copy-start.5 = (f32[256,2048]{1,0:T(8,128)S(1)}, f32[256,2048]{1,0:T(8,128)}, u32[]{:S(2)}) copy-start(f32[256,2048]{1,0:T(8,128)} %copy-done.4) | copy-start | bytes 6291460
  217.3 41.5 %copy-start.1 = (bf16[1280,1024]{1,0:T(8,128)(2,1)S(1)}, bf16[1280,1024]{1,0:T(8,128)(2,1)}, u32[]{:S(2)}) copy-start(bf16[1280,1024]{1,0:T(8,128)(2,1)} %param.15) | copy-start | bytes 7864324
